TPU v7x, 32 devices: a whole 2x2x4 slice. The times are simulated.
32 devices in a mesh: seq: 8 (over z, x), head: 4 (over y, core).
Axes of the slice: x: 2, y: 2, z: 4, core: 2. Of those that a mesh axis runs over, the one named last changes fastest.
Arguments:
- xs: bfloat16 [8192, 4096], P('seq', 'head'), may hold values from -6 to 6
- gate_branch: bfloat16 [8192, 4096], P('seq', 'head'), may hold values from -6 to 6
- bmat: bfloat16 [8192, 128], P('seq'), may hold values from -0.375 to 0.375
- cmat: bfloat16 [8192, 128], P('seq'), may hold values from -0.375 to 0.375
- dt_code: int32 [64, 8192], P('head', 'seq'), may hold values from 1 to 32768
- resets: int32 [8192], P('seq'), may hold values 0 or 1
- decay_rate: float32 [64], P('head'), may hold values from 4.8828125e-05 to 0.08, as said below
- skip: float32 [64], P('head'), may hold values from 0.5 to 1.5
- norm_gain: float32 [4096], P('head'), may hold values from 0.1 to 1.9
- out_weight: bfloat16 [4096, 4096], P('head'), may hold values from -0.09375 to 0.09375
Outputs:
- mixed: bfloat16 [8192, 4096], P(('seq', 'head'))
Inputs may be any that keep to these rules, and one draw needn't show every extreme that they name: `decay_rate`: positive rates.
All inputs are finite; a program needn't handle non-finite values. No bound on the sum of `resets` on one device may be relied on, other than what follows from the above.
Results may differ from a plain program's by a relative error of at most 0.023.
Values may be sent and summed in bfloat16 or wider, within the bound.
A program may use at most 128 MiB of HBM per device.

v0:
```python
import functools

import jax
import jax.numpy as jnp
from jax import lax
from jax.experimental import pallas as pl
from jax.experimental.pallas import tpu as pltpu
from jax.sharding import PartitionSpec as P

HEAD_DIM = 64
SPAN = 256
QUARTERS = 4
F32 = jnp.float32
BF16 = jnp.bfloat16
MESH = pl.DeviceIdType.MESH
VMEM_BYTES = 60 * 1024 * 1024


def dot_nt(a, b):
    return lax.dot_general(a, b, (((1,), (1,)), ((), ())), preferred_element_type=F32)


def dot_tn(a, b):
    return lax.dot_general(a, b, (((0,), (0,)), ((), ())), preferred_element_type=F32)


def dot_nn(a, b):
    return jnp.dot(a, b, preferred_element_type=F32)


def two_pieces(v):
    high = v.astype(BF16)
    low = (v - high.astype(F32)).astype(BF16)
    return jnp.concatenate([high, low], axis=1)


def spread(heads):
    rows = lax.broadcasted_iota(jnp.int32, (2 * heads, heads * HEAD_DIM), 0)
    columns = lax.broadcasted_iota(jnp.int32, (2 * heads, heads * HEAD_DIM), 1)
    own = (columns // HEAD_DIM == rows) | (columns // HEAD_DIM == rows - heads)
    return jnp.where(own, 1.0, 0.0).astype(BF16)


def digits(code, flags):
    low = code & 127
    middle = (code >> 7) & 127
    high = code >> 14
    extra = jnp.broadcast_to(flags, code.shape)
    rows = jnp.concatenate([low, middle, high, extra], axis=0)
    return rows.astype(F32).astype(BF16)


def joined(sums, heads, axis):
    def take(n):
        return lax.slice_in_dim(sums, n * heads, (n + 1) * heads, axis=axis)

    return (take(0) + 128.0 * take(1) + 16384.0 * take(2)), take(3)


def layer_kernel(
    shards, x_ref, gate_ref, b_ref, c_ref, code_ref, flag_ref, rate_ref, skip_ref, gain_ref, w_hbm, out_ref,
    w, ssm, reach, own, state, gone, final, other_final, decay, other_decay, came, passed, incoming,
    mine, kept, send1, recv1, send2, recv2, sq_send, sq_recv,
    w_sem, fs, fr, ds, dr, cs, cr, s1, r1, s2, r2, sqs, sqr,
):
    me = lax.axis_index("head")
    rank = lax.axis_index("seq")
    core = me % 2
    half = me // 2
    partner = half * 2 + (1 - core)
    across = (1 - half) * 2 + core
    diagonal = (1 - half) * 2 + (1 - core)
    odd = rank % 2
    twin = rank + 1 - 2 * odd
    ticks, inner = x_ref.shape
    heads = code_ref.shape[0]
    width = out_ref.shape[1] // QUARTERS
    blocks = ticks // SPAN
    pieces = heads // 2
    piece = inner // pieces

    def load(q):
        return pltpu.make_async_copy(w_hbm.at[:, pl.ds(q * width, width)], w.at[q], w_sem.at[q])

    for q in range(QUARTERS):
        load(q).start()

    @pl.when(rank < 2)
    def _():
        came[...] = jnp.zeros_like(came)

    barrier = pltpu.get_barrier_semaphore()
    for other in (partner, across, diagonal):
        pl.semaphore_signal(barrier, inc=1, device_id={"head": other}, device_id_type=MESH)
    for other in (twin, (rank + 2) % shards, (rank + shards - 2) % shards):
        pl.semaphore_signal(barrier, inc=1, device_id={"seq": other}, device_id_type=MESH)

    eye = spread(heads)
    rate_row = rate_ref[...]
    hi = lax.broadcasted_iota(jnp.int32, (heads, heads), 0)
    hj = lax.broadcasted_iota(jnp.int32, (heads, heads), 1)
    rate_col = jnp.sum(jnp.where(hi == hj, rate_row, 0.0), axis=1, keepdims=True)
    wide_skip = dot_nn(two_pieces(jnp.broadcast_to(skip_ref[...], (8, heads))), eye)[0:1]

    def scales(codes):
        return jnp.transpose(jnp.minimum(codes.astype(F32) / 16.0, 1.0))

    def local_final():
        parts = digits(code_ref[...], flag_ref[...])
        i = lax.broadcasted_iota(jnp.int32, (ticks, ticks), 0)
        j = lax.broadcasted_iota(jnp.int32, (ticks, ticks), 1)
        later = jnp.where(j > i, 1.0, 0.0).astype(BF16)
        after, seen = joined(dot_nt(later, parts), heads, 1)
        factor = jnp.where(seen == 0.0, jnp.exp(-rate_row * (after / 16.0)), 0.0)
        factor = factor * scales(code_ref[...])
        wide = dot_nn(two_pieces(factor), eye)
        weighted = (x_ref[...].astype(F32) * wide).astype(BF16)
        whole = dot_tn(weighted, b_ref[...])
        own[...] = whole
        final[...] = whole.astype(BF16)
        every = jnp.ones((whole.shape[1], ticks), BF16)
        total, resets = joined(dot_nt(parts, every), heads, 0)
        decay[...] = jnp.where(resets == 0.0, jnp.exp(-rate_col * (total / 16.0)), 0.0)

    def final_copy(q):
        rows = pl.ds(q * piece, piece)
        return pltpu.make_async_remote_copy(
            src_ref=final.at[rows], dst_ref=other_final.at[rows], send_sem=fs.at[q],
            recv_sem=fr.at[q], device_id={"seq": twin}, device_id_type=MESH,
        )

    def decay_copy():
        return pltpu.make_async_remote_copy(
            src_ref=decay, dst_ref=other_decay, send_sem=ds.at[0],
            recv_sem=dr.at[0], device_id={"seq": twin}, device_id_type=MESH,
        )

    def chain_copy(q):
        rows = pl.ds(q * piece, piece)
        return pltpu.make_async_remote_copy(
            src_ref=passed.at[rows], dst_ref=came.at[rows], send_sem=cs.at[q],
            recv_sem=cr.at[q], device_id={"seq": (rank + 2) % shards}, device_id_type=MESH,
        )

    local_final()
    pl.semaphore_wait(barrier, 6)
    decay_copy().start()
    for q in range(pieces):
        final_copy(q).start()

    state[...] = jnp.zeros_like(state)
    gone[...] = jnp.zeros_like(gone)

    def intra(block, _):
        start = pl.multiple_of(block * SPAN, SPAN)
        rows = pl.ds(start, SPAN)
        codes = code_ref[:, rows]
        parts = digits(codes, flag_ref[:, rows])
        i = lax.broadcasted_iota(jnp.int32, (SPAN, SPAN), 0)
        j = lax.broadcasted_iota(jnp.int32, (SPAN, SPAN), 1)
        upto = jnp.where(j <= i, 1.0, 0.0).astype(BF16)
        later = jnp.where(j > i, 1.0, 0.0).astype(BF16)
        sum_col, count_col = joined(dot_nt(upto, parts), heads, 1)
        after_col, seen_after = joined(dot_nt(later, parts), heads, 1)
        sum_row, count_row = joined(dot_nt(parts, upto), heads, 0)
        cum_col = -rate_row * (sum_col / 16.0)
        cum_row = -rate_col * (sum_row / 16.0)
        to_end = jnp.where(seen_after == 0.0, jnp.exp(-rate_row * (after_col / 16.0)), 0.0)
        from_start = jnp.where(count_col == 0.0, jnp.exp(cum_col), 0.0)
        last = jnp.where(
            count_col[SPAN - 1 : SPAN] == 0.0, jnp.exp(cum_col[SPAN - 1 : SPAN]), 0.0
        )
        x = x_ref[rows, :].astype(F32)
        scaled = (x * dot_nn(scales(codes).astype(BF16), eye[0:heads])).astype(BF16)
        b = b_ref[rows, :]
        c = c_ref[rows, :]
        linked = (count_col[:, 0:1] == count_row[0:1, :]) & (j <= i)
        cross = jnp.where(linked, dot_nt(c, b), 0.0)
        left = lax.broadcasted_iota(jnp.int32, (SPAN, 2 * HEAD_DIM), 1) < HEAD_DIM
        old = state[...]
        carried = dot_nt(c, old.astype(BF16)) * dot_nn(two_pieces(from_start), eye)
        carried = carried + wide_skip * x
        for pair in range(heads // 2):
            columns = slice(pair * 2 * HEAD_DIM, (pair + 1) * 2 * HEAD_DIM)
            both = scaled[:, columns]
            sides = []
            for h in (2 * pair, 2 * pair + 1):
                gap = jnp.minimum(cum_col[:, h : h + 1] - cum_row[h : h + 1, :], 0.0)
                scores = (jnp.exp(gap) * cross).astype(BF16)
                sides.append(dot_nn(scores, both))
            ssm[rows, columns] = jnp.where(left, sides[0], sides[1]) + carried[:, columns]
        weighted = (scaled.astype(F32) * dot_nn(two_pieces(to_end), eye)).astype(BF16)
        fresh = dot_tn(weighted, b)
        spread_last = two_pieces(jnp.broadcast_to(last, (128, heads))).astype(F32)
        state[...] = dot_tn(eye, jnp.transpose(spread_last).astype(BF16)) * old + fresh
        before = gone[0:1, :]
        broken = gone[1:2, :]
        whole = jnp.where(
            (count_col + broken) == 0.0, jnp.exp(-rate_row * ((sum_col + before) / 16.0)), 0.0
        )
        reach[rows, :] = two_pieces(whole)
        gone[0:1, :] = before + sum_col[SPAN - 1 : SPAN]
        gone[1:2, :] = broken + count_col[SPAN - 1 : SPAN]
        return 0

    lax.fori_loop(0, blocks - 1, intra, 0)

    decay_copy().wait_recv()
    odd_f = odd.astype(F32)
    even_f = 1.0 - odd_f
    ours = decay[...]
    theirs = other_decay[...]
    second_decay = odd_f * ours + even_f * theirs
    both_decay = ours * theirs
    step_decay = odd_f * theirs + even_f
    for q in range(pieces):
        final_copy(q).wait_recv()

        @pl.when(rank >= 2)
        def _():
            chain_copy(q).wait_recv()

        for h in range(2 * q, 2 * q + 2):
            rows = slice(h * HEAD_DIM, (h + 1) * HEAD_DIM)
            here = own[rows, :]
            there = other_final[rows, :].astype(F32)
            before = came[rows, :].astype(F32)
            first = odd_f * there + even_f * here
            second = odd_f * here + even_f * there
            total = second_decay[h : h + 1, :] * first + second
            passed[rows, :] = (both_decay[h : h + 1, :] * before + total).astype(BF16)
            incoming[rows, :] = (step_decay[h : h + 1, :] * before + odd_f * there).astype(BF16)

        @pl.when(rank < shards - 2)
        def _():
            chain_copy(q).start()

    lax.fori_loop(blocks - 1, blocks, intra, 0)
    start = incoming[...]

    def prepare(block, slot):
        rows = pl.ds(pl.multiple_of(block * SPAN, SPAN), SPAN)
        carried = dot_nt(c_ref[rows, :], start) * dot_nn(reach[rows, :], eye)
        gate = gate_ref[rows, :].astype(F32)
        gated = (ssm[rows, :] + carried) * (gate / (1.0 + jnp.exp(-gate)))
        mine[...] = (gated * gain_ref[...]).astype(BF16)
        square = gated * gated
        high = square.astype(BF16)
        low = (square - high.astype(F32)).astype(BF16)
        ones = jnp.ones((8, inner), BF16)
        sq_send[slot] = dot_nt(ones, high) + dot_nt(ones, low)

    def square_copy(slot, other):
        return pltpu.make_async_remote_copy(
            src_ref=sq_send.at[slot], dst_ref=sq_recv.at[slot], send_sem=sqs.at[slot],
            recv_sem=sqr.at[slot], device_id={"head": other}, device_id_type=MESH,
        )

    def to_partner(turn, q):
        return pltpu.make_async_remote_copy(
            src_ref=send1.at[turn, q], dst_ref=recv1.at[turn, q], send_sem=s1.at[turn, q],
            recv_sem=r1.at[turn, q], device_id={"head": partner}, device_id_type=MESH,
        )

    def to_across(q):
        return pltpu.make_async_remote_copy(
            src_ref=send2.at[q], dst_ref=recv2.at[q], send_sem=s2.at[q],
            recv_sem=r2.at[q], device_id={"head": across}, device_id_type=MESH,
        )

    prepare(diagonal, 0)
    square_copy(0, diagonal).start()
    for q in range(QUARTERS):
        load(q).wait()

    def first(q, _):
        send1[0, q] = dot_nn(mine[...], w[q]).astype(BF16)
        to_partner(0, q).start()
        return 0

    lax.fori_loop(0, QUARTERS, first, 0)
    prepare(across, 1)
    square_copy(1, across).start()

    def second(q, _):
        part = dot_nn(mine[...], w[q])
        to_partner(0, q).wait_recv()
        send2[q] = (part + recv1[0, q].astype(F32)).astype(BF16)
        to_across(q).start()
        return 0

    lax.fori_loop(0, QUARTERS, second, 0)
    prepare(partner, 2)
    square_copy(2, partner).start()

    def third(q, _):
        send1[1, q] = dot_nn(mine[...], w[q]).astype(BF16)
        to_partner(1, q).start()
        return 0

    lax.fori_loop(0, QUARTERS, third, 0)
    prepare(me, 3)

    def fourth(q, _):
        part = dot_nn(mine[...], w[q])
        to_partner(1, q).wait_recv()
        kept[q] = part + recv1[1, q].astype(F32)
        return 0

    lax.fori_loop(0, QUARTERS, fourth, 0)
    for slot, other in enumerate((diagonal, across, partner)):
        square_copy(slot, other).wait()
    total = (sq_send[3] + sq_recv[0] + sq_recv[1] + sq_recv[2])[0:1, :]
    norm = lax.rsqrt(total / (4 * inner) + 1e-05)
    i = lax.broadcasted_iota(jnp.int32, (SPAN, SPAN), 0)
    j = lax.broadcasted_iota(jnp.int32, (SPAN, SPAN), 1)
    column = jnp.sum(jnp.where(i == j, norm, 0.0), axis=1, keepdims=True)
    for q in range(QUARTERS):
        to_across(q).wait_recv()
        out_ref[:, q * width : (q + 1) * width] = (
            (kept[q] + recv2[q].astype(F32)) * column
        ).astype(BF16)
    for q in range(QUARTERS):
        to_partner(0, q).wait_send()
        to_partner(1, q).wait_send()
        to_across(q).wait_send()
    for q in range(pieces):
        final_copy(q).wait_send()
    decay_copy().wait_send()

    @pl.when(rank < shards - 2)
    def _():
        for q in range(pieces):
            chain_copy(q).wait_send()


def local(shards, xs, gate_branch, bmat, cmat, dt_code, resets, decay_rate, skip, norm_gain, out_weight):
    ticks, inner = xs.shape
    heads = dt_code.shape[0]
    size = bmat.shape[1]
    model = out_weight.shape[1]
    width = model // QUARTERS
    pieces = heads // 2
    vmem = pl.BlockSpec(memory_space=pltpu.VMEM)
    dma = pltpu.SemaphoreType.DMA
    return pl.pallas_call(
        functools.partial(layer_kernel, shards),
        out_shape=jax.ShapeDtypeStruct((SPAN, model), BF16),
        in_specs=[vmem] * 9 + [pl.BlockSpec(memory_space=pl.ANY)],
        out_specs=vmem,
        scratch_shapes=[
            pltpu.VMEM((QUARTERS, inner, width), BF16),
            pltpu.VMEM((ticks, inner), F32),
            pltpu.VMEM((ticks, 2 * heads), BF16),
            pltpu.VMEM((inner, size), F32),
            pltpu.VMEM((inner, size), F32),
            pltpu.VMEM((8, heads), F32),
            pltpu.VMEM((inner, size), BF16),
            pltpu.VMEM((inner, size), BF16),
            pltpu.VMEM((heads, size), F32),
            pltpu.VMEM((heads, size), F32),
            pltpu.VMEM((inner, size), BF16),
            pltpu.VMEM((inner, size), BF16),
            pltpu.VMEM((inner, size), BF16),
            pltpu.VMEM((SPAN, inner), BF16),
            pltpu.VMEM((QUARTERS, SPAN, width), F32),
            pltpu.VMEM((2, QUARTERS, SPAN, width), BF16),
            pltpu.VMEM((2, QUARTERS, SPAN, width), BF16),
            pltpu.VMEM((QUARTERS, SPAN, width), BF16),
            pltpu.VMEM((QUARTERS, SPAN, width), BF16),
            pltpu.VMEM((4, 8, SPAN), F32),
            pltpu.VMEM((3, 8, SPAN), F32),
            dma((QUARTERS,)),
            dma((pieces,)),
            dma((pieces,)),
            dma((1,)),
            dma((1,)),
            dma((pieces,)),
            dma((pieces,)),
            dma((2, QUARTERS)),
            dma((2, QUARTERS)),
            dma((QUARTERS,)),
            dma((QUARTERS,)),
            dma((3,)),
            dma((3,)),
        ],
        compiler_params=pltpu.CompilerParams(
            collective_id=0, has_side_effects=True, vmem_limit_bytes=VMEM_BYTES
        ),
        name="layer",
    )(
        xs, gate_branch, bmat, cmat, dt_code, resets[None, :], decay_rate[None, :], skip[None, :],
        norm_gain[None, :], out_weight,
    )


def solution(mesh):
    in_specs = (
        P("seq", "head"),
        P("seq", "head"),
        P("seq", None),
        P("seq", None),
        P("head", "seq"),
        P("seq"),
        P("head"),
        P("head"),
        P("head"),
        P("head", None),
    )
    out_specs = P(("seq", "head"), None)
    return jax.shard_map(
        functools.partial(local, mesh.shape["seq"]),
        mesh=mesh, in_specs=in_specs, out_specs=out_specs, check_vma=False,
    )
```

profile of v0, /device:TPU:26, one launch (start us, length us, event | category | flops | bytes accessed | tf_op | source)
XLA Modules:
  0.0 84.6 jit_solution(7948976412170406140)
XLA Ops:
  0.0 81.5 %layer.1 = bf16[256,4096]{1,0:T(8,128)(2,1)} custom-call(bf16[1024,1024]{1,0:T(8,128)(2,1)} %x_ref.1, bf16[1024,1024]{1,0:T(8,128)(2,1)} %gate_ref.1, bf16[1024,128]{1,0:T(8,128)(2,1)} %b_ref.1, bf16[1024,128]{1,0:T(8,128)(2,1)} %c_ref.1, s32[16,1024]{1,0:T(8,128)} %code_ref.1, s32[1,1024]{1,0:T(1,128)} %bitcast.4, f32[1,16]{1,0:T(1,128)} %bitcast.6, ...), custom_call_target="tpu_custom_call" | custom-call | tf_op jit(solution)/shard_map/layer/pallas_call | solution.py:346
  81.5 3.1 %copy.12 = bf16[256,4096]{1,0:T(8,128)(2,1)} copy(bf16[256,4096]{1,0:T(8,128)(2,1)} %layer.1) | data formatting | bytes 4194304
where the time goes:
time: 84.8 us; the launch traced here: 84.6 us
  Pallas kernels  81.5 us (96%)
  local copies, waits for them, and re-layouts  3.13 us (4%)
    pallas_call x1, Pallas kernels, local(): pl.pallas_call(functools.partial(layer_kernel, shards), out_shape=jax.Sha...  81.5 us
    unnamed x1, local copies, waits for them, and re-layouts  3.13 us

commit v1 on v0

v1 whole, which is shorter than its diff:
```python
import functools

import jax
import jax.numpy as jnp
from jax import lax
from jax.experimental import pallas as pl
from jax.experimental.pallas import tpu as pltpu
from jax.sharding import PartitionSpec as P

HEAD_DIM = 64
SPAN = 256
CHUNKS = 8
EARLY = 3
F32 = jnp.float32
BF16 = jnp.bfloat16
MESH = pl.DeviceIdType.MESH
VMEM_BYTES = 60 * 1024 * 1024
LOG2E = 1.4426950408889634


def dot_nt(a, b):
    return lax.dot_general(a, b, (((1,), (1,)), ((), ())), preferred_element_type=F32)


def dot_tn(a, b):
    return lax.dot_general(a, b, (((0,), (0,)), ((), ())), preferred_element_type=F32)


def dot_nn(a, b):
    return jnp.dot(a, b, preferred_element_type=F32)


def two_pieces(v):
    high = v.astype(BF16)
    low = (v - high.astype(F32)).astype(BF16)
    return jnp.concatenate([high, low], axis=1)


def spread(heads):
    rows = lax.broadcasted_iota(jnp.int32, (2 * heads, heads * HEAD_DIM), 0)
    columns = lax.broadcasted_iota(jnp.int32, (2 * heads, heads * HEAD_DIM), 1)
    own = (columns // HEAD_DIM == rows) | (columns // HEAD_DIM == rows - heads)
    return jnp.where(own, 1.0, 0.0).astype(BF16)


def digits(code, flags):
    low = code & 127
    middle = (code >> 7) & 127
    high = code >> 14
    extra = jnp.broadcast_to(flags, code.shape)
    rows = jnp.concatenate([low, middle, high, extra], axis=0)
    return rows.astype(F32).astype(BF16)


def joined(sums, heads, axis):
    def take(n):
        return lax.slice_in_dim(sums, n * heads, (n + 1) * heads, axis=axis)

    return (take(0) + 128.0 * take(1) + 16384.0 * take(2)), take(3)


def layer_kernel(
    shards, x_hbm, gate_hbm, b_ref, c_ref, code_ref, flag_ref, rate_ref, skip_ref, gain_ref, w_hbm, out_ref,
    x_ref, gate_ref, w, scaled, cross, columns_of, rows_of, fall, eyes, skips, gains, reach, local, ssm, mine, squares,
    own, final, other_final, decay, other_decay, came, passed, starts,
    kept, send1, recv1, send2, recv2, sq_send, sq_recv,
    x_sem, g_sem, w_sem, fs, fr, ds, dr, cs, cr, s1, r1, s2, r2, sqs, sqr,
):
    me = lax.axis_index("head")
    rank = lax.axis_index("seq")
    core = me % 2
    half = me // 2
    partner = half * 2 + (1 - core)
    across = (1 - half) * 2 + core
    diagonal = (1 - half) * 2 + (1 - core)
    odd = rank % 2
    twin = rank + 1 - 2 * odd
    level = rank // 2
    ticks, inner = x_ref.shape
    heads = code_ref.shape[0]
    width = out_ref.shape[1] // CHUNKS
    blocks = ticks // SPAN
    pieces = heads // 2
    lanes = 2 * HEAD_DIM
    lower = SPAN // 2

    def load_x(n):
        rows = pl.ds(n * SPAN, SPAN)
        return pltpu.make_async_copy(x_hbm.at[rows], x_ref.at[rows], x_sem.at[n])

    def load_gate(n):
        rows = pl.ds(n * SPAN, SPAN)
        return pltpu.make_async_copy(gate_hbm.at[rows], gate_ref.at[rows], g_sem.at[n])

    def load(n):
        return pltpu.make_async_copy(w_hbm.at[:, pl.ds(n * width, width)], w.at[n], w_sem.at[n])

    for n in range(blocks):
        load_x(n).start()
    for n in range(blocks):
        load_gate(n).start()
    for n in range(CHUNKS):
        load(n).start()

    barrier = pltpu.get_barrier_semaphore()
    for other in (partner, across, diagonal):
        pl.semaphore_signal(barrier, inc=1, device_id={"head": other}, device_id_type=MESH)
    for other in (twin, (rank + 2) % shards, (rank + shards - 2) % shards):
        pl.semaphore_signal(barrier, inc=1, device_id={"seq": other}, device_id_type=MESH)

    eye = spread(heads)
    rate_row = rate_ref[...] * (LOG2E / 16.0)
    hi = lax.broadcasted_iota(jnp.int32, (heads, heads), 0)
    hj = lax.broadcasted_iota(jnp.int32, (heads, heads), 1)
    rate_col = jnp.sum(jnp.where(hi == hj, rate_row, 0.0), axis=1, keepdims=True)
    si = lax.broadcasted_iota(jnp.int32, (SPAN, SPAN), 0)
    sj = lax.broadcasted_iota(jnp.int32, (SPAN, SPAN), 1)

    def scales(codes):
        return jnp.transpose(jnp.minimum(codes.astype(F32) / 16.0, 1.0))

    def local_states():
        ti = lax.broadcasted_iota(jnp.int32, (SPAN + 8, SPAN), 0)
        tj = lax.broadcasted_iota(jnp.int32, (SPAN + 8, SPAN), 1)
        later = jnp.where((tj > ti) | (ti >= SPAN), 1.0, 0.0).astype(BF16)
        factors, last = [], []
        for n in range(blocks):
            tokens = slice(n * SPAN, (n + 1) * SPAN)
            codes = code_ref[:, tokens]
            after, seen = joined(dot_nt(later, digits(codes, flag_ref[:, tokens])), heads, 1)
            kept_on = jnp.where(seen == 0.0, jnp.exp2(-rate_row * after), 0.0)
            factors.append(kept_on[0:SPAN] * scales(codes))
            last.append(kept_on[SPAN : SPAN + 1])
        so_far = [jnp.ones_like(last[0])]
        for n in range(blocks):
            so_far.append(so_far[-1] * last[n])
        stack = so_far + last
        stack = stack + [so_far[0]] * (16 - len(stack))
        wide_rows = dot_nn(two_pieces(jnp.concatenate(stack, axis=0)), eye)
        state = None
        for n in range(blocks):
            tokens = slice(n * SPAN, (n + 1) * SPAN)
            wide = dot_nn(two_pieces(factors[n]), eye)
            load_x(n).wait()
            weighted = (x_ref[tokens, :].astype(F32) * wide).astype(BF16)
            fresh = dot_tn(b_ref[tokens, :], weighted)
            if n > 0:
                for q in range(pieces):
                    local[n, q] = state[:, q * lanes : (q + 1) * lanes]
                fresh = fresh + wide_rows[blocks + 1 + n : blocks + 2 + n] * state
            state = fresh
        for q in range(pieces):
            part = slice(q * lanes, (q + 1) * lanes)
            own[q] = state[:, part]
            final[q] = state[:, part].astype(BF16)
            local[0, q] = jnp.zeros((local.shape[2], lanes), F32)
            decay[q] = wide_rows[blocks : blocks + 1, part]
            for n in range(blocks):
                reach[n, q] = wide_rows[n : n + 1, part]

    def final_copy(q):
        return pltpu.make_async_remote_copy(
            src_ref=final.at[q], dst_ref=other_final.at[q], send_sem=fs.at[q],
            recv_sem=fr.at[q], device_id={"seq": twin}, device_id_type=MESH,
        )

    def decay_copy():
        return pltpu.make_async_remote_copy(
            src_ref=decay, dst_ref=other_decay, send_sem=ds.at[0],
            recv_sem=dr.at[0], device_id={"seq": twin}, device_id_type=MESH,
        )

    def chain_copy(q):
        return pltpu.make_async_remote_copy(
            src_ref=passed.at[q], dst_ref=came.at[q], send_sem=cs.at[q],
            recv_sem=cr.at[q], device_id={"seq": (rank + 2) % shards}, device_id_type=MESH,
        )

    def square_copy(slot, other):
        return pltpu.make_async_remote_copy(
            src_ref=sq_send.at[slot], dst_ref=sq_recv.at[slot], send_sem=sqs.at[slot],
            recv_sem=sqr.at[slot], device_id={"head": other}, device_id_type=MESH,
        )

    def to_partner(turn, n):
        return pltpu.make_async_remote_copy(
            src_ref=send1.at[turn, n], dst_ref=recv1.at[turn, n], send_sem=s1.at[turn, n],
            recv_sem=r1.at[turn, n], device_id={"head": partner}, device_id_type=MESH,
        )

    def to_across(n):
        return pltpu.make_async_remote_copy(
            src_ref=send2.at[n], dst_ref=recv2.at[n], send_sem=s2.at[n],
            recv_sem=r2.at[n], device_id={"head": across}, device_id_type=MESH,
        )

    def block_of(slot):
        turn = slot // 2
        side = slot % 2
        row = (1 - turn) * (1 - half) + turn * half
        return row * 2 + (1 - side) * (1 - core) + side * core

    def rows_at(slot):
        return pl.ds(pl.multiple_of(block_of(slot) * SPAN, SPAN), SPAN)

    def columns_at(q):
        return pl.ds(pl.multiple_of(q * lanes, lanes), lanes)

    with jax.named_scope("A_local"):
        local_states()
    with jax.named_scope("B_barrier"):
        pl.semaphore_wait(barrier, 6)
    decay_copy().start()
    for q in range(pieces):
        final_copy(q).start()

    @pl.when(rank < 2)
    def _():
        came[...] = jnp.zeros_like(came)

    wide_skip = dot_nn(two_pieces(jnp.broadcast_to(skip_ref[...], (8, heads))), eye)[0:1]
    for q in range(pieces):
        part = slice(q * lanes, (q + 1) * lanes)
        eyes[q] = eye[:, part]
        skips[q] = wide_skip[:, part]
        gains[q] = gain_ref[:, part]
    squares[...] = jnp.zeros_like(squares)

    def tables(slot, _):
        rows = rows_at(slot)
        codes = code_ref[:, rows]
        parts = digits(codes, flag_ref[:, rows])
        upto = jnp.where(sj <= si, 1.0, 0.0).astype(BF16)
        sum_col, count_col = joined(dot_nt(upto, parts), heads, 1)
        sum_row, count_row = joined(dot_nt(parts, upto), heads, 0)
        cum_col = -rate_row * sum_col
        cum_row = -rate_col * sum_row
        for q in range(pieces):
            columns_of[slot, q] = cum_col[:, 2 * q : 2 * q + 2]
        for h in range(heads):
            rows_of[slot, h] = cum_row[h : h + 1, :]
        fall[slot] = two_pieces(jnp.where(count_col == 0.0, jnp.exp2(cum_col), 0.0))
        linked = (count_col[:, 0:1] == count_row[0:1, :]) & (sj <= si)
        cross[slot] = jnp.where(linked, dot_nt(c_ref[rows, :], b_ref[rows, :]), 0.0)
        wide = dot_nn(scales(codes).astype(BF16), eye[0:heads])
        scaled[rows, :] = (x_ref[rows, :].astype(F32) * wide).astype(BF16)
        return 0

    def intra(slot, q):
        both = scaled[rows_at(slot), columns_at(q)]
        lane = lax.broadcasted_iota(jnp.int32, (1, lanes), 1)
        left = jnp.where(lane < HEAD_DIM, 1.0, 0.0).astype(BF16)
        sides = (both * left, both * (1.0 - left))
        pair = columns_of[slot, q]
        upper, under = [], []
        for side in range(2):
            column = pair[:, side : side + 1]
            row = rows_of[slot, 2 * q + side]
            gap = jnp.minimum(column[0:lower] - row[:, 0:lower], 0.0)
            upper.append((jnp.exp2(gap) * cross[slot, 0:lower, 0:lower]).astype(BF16))
            gap = jnp.minimum(column[lower:] - row, 0.0)
            under.append((jnp.exp2(gap) * cross[slot, lower:, :]).astype(BF16))
        top = dot_nn(
            jnp.concatenate(upper, axis=1),
            jnp.concatenate([sides[0][0:lower], sides[1][0:lower]], axis=0),
        )
        bottom = dot_nn(jnp.concatenate(under, axis=1), jnp.concatenate(sides, axis=0))
        return jnp.concatenate([top, bottom], axis=0)

    def finish(slot, q, within):
        rows = rows_at(slot)
        part = columns_at(q)
        carried = dot_nn(c_ref[rows, :], starts[block_of(slot), q]) * dot_nn(fall[slot], eyes[q])
        gate = gate_ref[rows, part].astype(F32)
        total = within + carried + skips[q] * x_ref[rows, part].astype(F32)
        gated = total * (gate / (1.0 + jnp.exp(-gate)))
        mine[slot, :, part] = (gated * gains[q]).astype(BF16)
        squares[slot] = squares[slot] + gated * gated

    def send_squares(slot):
        value = squares[slot]
        high = value.astype(BF16)
        low = (value - high.astype(F32)).astype(BF16)
        ones = jnp.ones((8, lanes), BF16)
        sq_send[slot] = dot_nt(ones, high) + dot_nt(ones, low)

    def early(q, _):
        ssm[0, q] = intra(0, q)
        ssm[1, q] = intra(1, q)
        return 0

    with jax.named_scope("C_tables"):
        lax.fori_loop(0, 2, tables, 0)
    later_level = (level + shards) // (shards + 1)
    with jax.named_scope("D_early"):
        lax.fori_loop(0, EARLY + (pieces - EARLY) * later_level, early, 0)

    with jax.named_scope("E_decay"):
        decay_copy().wait_recv()
    for n in range(blocks):
        load_gate(n).wait()
    odd_f = odd.astype(F32)
    even_f = 1.0 - odd_f

    def chain(q, _):
        final_copy(q).wait_recv()

        @pl.when(rank >= 2)
        def _():
            chain_copy(q).wait_recv()

        ours = decay[q]
        theirs = other_decay[q]
        here = own[q]
        there = other_final[q].astype(F32)
        before = came[q].astype(F32)
        first = odd_f * there + even_f * here
        second = odd_f * here + even_f * there
        total = (odd_f * ours + even_f * theirs) * first + second
        passed[q] = (ours * theirs * before + total).astype(BF16)

        @pl.when(rank < shards - 2)
        def _():
            chain_copy(q).start()

        incoming = (odd_f * theirs + even_f) * before + odd_f * there
        for n in range(blocks):
            starts[n, q] = (local[n, q] + reach[n, q] * incoming).astype(BF16)

        @pl.when((level < 1) & (q < pieces - EARLY))
        def _():
            early(EARLY + q, 0)

        finish(0, q, ssm[0, q])
        finish(1, q, ssm[1, q])
        return 0

    with jax.named_scope("F_chain"):
        lax.fori_loop(0, pieces, chain, 0)
    with jax.named_scope("G_wload"):
        for n in range(CHUNKS):
            load(n).wait()

    def give(n):
        send1[0, n] = dot_nn(mine[0], w[n]).astype(BF16)
        to_partner(0, n).start()

    def cross_over(n):
        part = dot_nn(mine[1], w[n])
        with jax.named_scope("H_w"):
            to_partner(0, n).wait_recv()
        send2[n] = (part + recv1[0, n].astype(F32)).astype(BF16)
        to_across(n).start()

    def first(n, _):
        give(n)
        cross_over(n - 1)
        return 0

    with jax.named_scope("H_first"):
        give(0)
        lax.fori_loop(1, CHUNKS, first, 0)
        cross_over(CHUNKS - 1)
    send_squares(0)
    square_copy(0, diagonal).start()
    send_squares(1)
    square_copy(1, across).start()

    def rest(q, _):
        within = (intra(2, q), intra(3, q))
        finish(2, q, within[0])
        finish(3, q, within[1])
        return 0

    with jax.named_scope("I_rest"):
        lax.fori_loop(2, 4, tables, 0)
        lax.fori_loop(0, pieces, rest, 0)
    send_squares(2)
    square_copy(2, partner).start()
    send_squares(3)

    def third(n, _):
        send1[1, n] = dot_nn(mine[2], w[n]).astype(BF16)
        to_partner(1, n).start()
        return 0

    def fourth(n, _):
        part = dot_nn(mine[3], w[n])
        to_partner(1, n).wait_recv()
        kept[n] = part + recv1[1, n].astype(F32)
        return 0

    with jax.named_scope("J_third"):
        lax.fori_loop(0, CHUNKS, third, 0)
    with jax.named_scope("K_fourth"):
        lax.fori_loop(0, CHUNKS, fourth, 0)
    for slot, other in enumerate((diagonal, across, partner)):
        square_copy(slot, other).wait()
    total = (sq_send[3] + sq_recv[0] + sq_recv[1] + sq_recv[2])[0:1, :]
    norm = lax.rsqrt(total / (4 * inner) + 1e-05)
    column = jnp.sum(jnp.where(si == sj, norm, 0.0), axis=1, keepdims=True)
    for n in range(CHUNKS):
        with jax.named_scope("Q_across"):
            to_across(n).wait_recv()
        out_ref[:, n * width : (n + 1) * width] = (
            (kept[n] + recv2[n].astype(F32)) * column
        ).astype(BF16)
    for n in range(CHUNKS):
        to_partner(0, n).wait_send()
        to_partner(1, n).wait_send()
        to_across(n).wait_send()
    for q in range(pieces):
        final_copy(q).wait_send()
    decay_copy().wait_send()

    @pl.when(rank < shards - 2)
    def _():
        for q in range(pieces):
            chain_copy(q).wait_send()


def local(shards, xs, gate_branch, bmat, cmat, dt_code, resets, decay_rate, skip, norm_gain, out_weight):
    ticks, inner = xs.shape
    heads = dt_code.shape[0]
    size = bmat.shape[1]
    model = out_weight.shape[1]
    width = model // CHUNKS
    pieces = heads // 2
    blocks = ticks // SPAN
    lanes = 2 * HEAD_DIM
    vmem = pl.BlockSpec(memory_space=pltpu.VMEM)
    anywhere = pl.BlockSpec(memory_space=pl.ANY)
    dma = pltpu.SemaphoreType.DMA
    return pl.pallas_call(
        functools.partial(layer_kernel, shards),
        out_shape=pltpu.VMEM((SPAN, model), BF16),
        in_specs=[anywhere, anywhere] + [vmem] * 7 + [anywhere],
        out_specs=vmem,
        scratch_shapes=[
            pltpu.VMEM((ticks, inner), BF16),
            pltpu.VMEM((ticks, inner), BF16),
            pltpu.VMEM((CHUNKS, inner, width), BF16),
            pltpu.VMEM((ticks, inner), BF16),
            pltpu.VMEM((4, SPAN, SPAN), F32),
            pltpu.VMEM((4, pieces, SPAN, 2), F32),
            pltpu.VMEM((4, heads, 1, SPAN), F32),
            pltpu.VMEM((4, SPAN, 2 * heads), BF16),
            pltpu.VMEM((pieces, 2 * heads, lanes), BF16),
            pltpu.VMEM((pieces, 1, lanes), F32),
            pltpu.VMEM((pieces, 1, lanes), F32),
            pltpu.VMEM((blocks, pieces, 1, lanes), F32),
            pltpu.VMEM((blocks, pieces, size, lanes), F32),
            pltpu.VMEM((2, pieces, SPAN, lanes), F32),
            pltpu.VMEM((4, SPAN, inner), BF16),
            pltpu.VMEM((4, SPAN, lanes), F32),
            pltpu.VMEM((pieces, size, lanes), F32),
            pltpu.VMEM((pieces, size, lanes), BF16),
            pltpu.VMEM((pieces, size, lanes), BF16),
            pltpu.VMEM((pieces, 1, lanes), F32),
            pltpu.VMEM((pieces, 1, lanes), F32),
            pltpu.VMEM((pieces, size, lanes), BF16),
            pltpu.VMEM((pieces, size, lanes), BF16),
            pltpu.VMEM((blocks, pieces, size, lanes), BF16),
            pltpu.VMEM((CHUNKS, SPAN, width), F32),
            pltpu.VMEM((2, CHUNKS, SPAN, width), BF16),
            pltpu.VMEM((2, CHUNKS, SPAN, width), BF16),
            pltpu.VMEM((CHUNKS, SPAN, width), BF16),
            pltpu.VMEM((CHUNKS, SPAN, width), BF16),
            pltpu.VMEM((4, 8, SPAN), F32),
            pltpu.VMEM((3, 8, SPAN), F32),
            dma((blocks,)),
            dma((blocks,)),
            dma((CHUNKS,)),
            dma((pieces,)),
            dma((pieces,)),
            dma((1,)),
            dma((1,)),
            dma((pieces,)),
            dma((pieces,)),
            dma((2, CHUNKS)),
            dma((2, CHUNKS)),
            dma((CHUNKS,)),
            dma((CHUNKS,)),
            dma((3,)),
            dma((3,)),
        ],
        compiler_params=pltpu.CompilerParams(
            collective_id=0, has_side_effects=True, vmem_limit_bytes=VMEM_BYTES
        ),
        name="layer",
    )(
        xs, gate_branch, bmat, cmat, dt_code, resets[None, :], decay_rate[None, :], skip[None, :],
        norm_gain[None, :], out_weight,
    )


def solution(mesh):
    in_specs = (
        P("seq", "head"),
        P("seq", "head"),
        P("seq", None),
        P("seq", None),
        P("head", "seq"),
        P("seq"),
        P("head"),
        P("head"),
        P("head"),
        P("head", None),
    )
    out_specs = P(("seq", "head"), None)
    return jax.shard_map(
        functools.partial(local, mesh.shape["seq"]),
        mesh=mesh, in_specs=in_specs, out_specs=out_specs, check_vma=False,
    )
```

time: 84.8 us -> 74.1 us (0.87)
  Pallas kernels: 81.5 us -> 72 us
  local copies, waits for them, and re-layouts: 3.13 us -> 1.32 us
    pallas_call x1, Pallas kernels: 81.5 us -> 72 us  [local(): pl.pallas_call(functools.partial(layer_kernel, shards), out_shape=pltpu.V...]
    unnamed x1, local copies, waits for them, and re-layouts: 3.13 us -> 1.32 us
where the time goes in v1:
time: 74.1 us; the launch traced here: 73.3 us
  Pallas kernels  72 us (97%)
  local copies, waits for them, and re-layouts  1.32 us (2%)
    pallas_call x1, Pallas kernels, local(): pl.pallas_call(functools.partial(layer_kernel, shards), out_shape=pltpu.V...  72 us

profile of v1, /device:TPU:26, one launch (start us, length us, event | category | flops | bytes accessed | tf_op | source)
XLA Modules:
  0.0 73.3 jit_solution(11239192521395462105)
XLA Ops:
  0.0 72.0 %layer.1 = bf16[256,4096]{1,0:T(8,128)(2,1)S(1)} custom-call(bf16[1024,1024]{1,0:T(8,128)(2,1)} %x_hbm.1, bf16[1024,1024]{1,0:T(8,128)(2,1)} %gate_hbm.1, bf16[1024,128]{1,0:T(8,128)(2,1)} %b_ref.1, bf16[1024,128]{1,0:T(8,128)(2,1)} %c_ref.1, s32[16,1024]{1,0:T(8,128)} %code_ref.1, s32[1,1024]{1,0:T(1,128)} %bitcast.4, f32[1,16]{1,0:T(1,128)} %bitcast.6, ...), custom_call_target="tpu_custom_call" | custom-call | tf_op jit(solution)/shard_map/layer/pallas_call | solution.py:434
  72.0 1.3 %copy.12 = bf16[256,4096]{1,0:T(8,128)(2,1)} copy(bf16[256,4096]{1,0:T(8,128)(2,1)S(1)} %layer.1) | data formatting | bytes 4194304
